TPU v7x, 32 devices: a whole 2x2x4 slice. The times are simulated.
32 devices in a mesh: dp: 8 (over y, x, core), mp: 4 (over z).
Axes of the slice: x: 2, y: 2, z: 4, core: 2. Of those that a mesh axis runs over, the one named last changes fastest.
Arguments:
- history_sequences: float32 [64, 512], P('dp'), may hold values from -65 to 65, as said below
- later_steps: float32 [64, 128], P('dp'), may hold values from -65 to 65
- patch_lift_matrix: bfloat16 [32, 1280], P(None, 'dp'), may hold values from -1 to 1
- scaling_factors: bfloat16 [2, 1280], P(None, 'dp'), may hold values from 0.5 to 1.5
- asking_matrix: bfloat16 [1280, 1280], P('dp', 'mp'), may hold values from -0.15625 to 0.15625
- lookup_matrix: bfloat16 [1280, 1280], P('dp', 'mp'), may hold values from -0.15625 to 0.15625
- content_matrix: bfloat16 [1280, 1280], P('dp', 'mp'), may hold values from -0.15625 to 0.15625
- attend_exit_matrix: bfloat16 [1280, 1280], P('mp', 'dp'), may hold values from -0.15625 to 0.15625
- outlook_matrix: bfloat16 [1280, 1280], P('dp', 'mp'), may hold values from -0.15625 to 0.15625
Outputs:
- loss_mean: float32 [], replicated
- embed_grad: float32 [32, 1280], P(None, 'dp')
- gains_grad: float32 [2, 1280], P(None, 'dp')
- query_grad: float32 [1280, 1280], P('dp', 'mp')
- key_grad: float32 [1280, 1280], P('dp', 'mp')
- value_grad: float32 [1280, 1280], P('dp', 'mp')
- output_grad: float32 [1280, 1280], P('mp', 'dp')
- head_weight_gradient: float32 [1280, 1280], P('dp', 'mp')
Inputs may be any that keep to these rules, and one draw needn't show every extreme that they name: `history_sequences`: later_steps continues the history of each series.
All inputs are finite; a program needn't handle non-finite values.
Results may differ from a plain program's by a relative error of at most 0.005.
Values may be sent and summed in bfloat16 or wider, within the bound.
A program may use at most 64 MiB of HBM per device.

v0:
```python
import math

import jax
import jax.numpy as jnp
from jax import lax
from jax.sharding import PartitionSpec as P

PATCH = 32
HORIZON_SPAN = 128
PATCHES = 16
LEVEL_CHANNELS = 10
HEAD_DIM = 80


EPS = 1e-06
STAT_EPS = 1e-05
SMOOTHING_RADIUS = 0.05


def rms_forward(residual, gain):
    factor = lax.rsqrt(jnp.mean(residual * residual, axis=1, keepdims=True) + EPS)
    return ((residual * factor * gain[None, :]).astype(jnp.bfloat16), factor)


def rms_backward(residual, factor, gain, upstream):
    weighted = gain[None, :] * upstream
    inner = jnp.mean(weighted * residual, axis=1, keepdims=True)
    back = factor * weighted - residual * factor * factor * factor * inner
    gain_term = jnp.sum(upstream * residual * factor, axis=0)
    return (back, gain_term)


def positions(length, width):
    half = width // 2
    freqs = jnp.exp(-math.log(10000.0) * jnp.arange(half, dtype=jnp.float32) / half)
    angles = jnp.arange(length, dtype=jnp.float32)[:, None] * freqs[None, :]
    return jnp.concatenate([jnp.sin(angles), jnp.cos(angles)], axis=1)


def prepare(history_sequences, later_steps):
    number = history_sequences.shape[0]
    centre = jnp.mean(history_sequences, axis=1, keepdims=True)
    spread = jnp.sqrt(
        jnp.mean((history_sequences - centre) * (history_sequences - centre), axis=1, keepdims=True)
        + STAT_EPS
    )
    normed = (history_sequences - centre) / spread
    ahead = (later_steps - centre) / spread
    joined = jnp.concatenate([normed, ahead], axis=1).reshape(number, -1, PATCH)
    reach = later_steps.shape[1] // PATCH
    future_values = jnp.concatenate(
        [joined[:, offset + 1 : offset + 1 + PATCHES] for offset in range(reach)], axis=2
    )
    future_values = future_values.reshape(number * PATCHES, reach * PATCH)
    patches = normed.reshape(number * PATCHES, PATCH).astype(jnp.bfloat16)
    return (patches, future_values)


def attention_forward(queries, keys, values, number):
    layout = (number, PATCHES, -1, HEAD_DIM)
    query_blocks = queries.reshape(layout)
    key_blocks = keys.reshape(layout)
    value_blocks = values.reshape(layout)
    scale = 1.0 / math.sqrt(HEAD_DIM)
    scores = (
        jnp.einsum("sihd,sjhd->shij", query_blocks, key_blocks, preferred_element_type=jnp.float32)
        * scale
    )
    place = jnp.arange(PATCHES)
    causal = place[:, None] >= place[None, :]
    raised = jnp.where(causal, jnp.exp(scores), 0.0)
    probs = raised / jnp.sum(raised, axis=3, keepdims=True)
    probs_low = probs.astype(jnp.bfloat16)
    context = jnp.einsum(
        "shij,sjhd->sihd", probs_low, value_blocks, preferred_element_type=jnp.float32
    )
    context = context.astype(jnp.bfloat16).reshape(number * PATCHES, -1)
    return (context, probs, probs_low)


def attention_backward(context_grad, queries, keys, values, probs, probs_low, number):
    layout = (number, PATCHES, -1, HEAD_DIM)
    query_blocks = queries.reshape(layout)
    key_blocks = keys.reshape(layout)
    value_blocks = values.reshape(layout)
    grad_blocks = context_grad.reshape(layout)
    scale = 1.0 / math.sqrt(HEAD_DIM)
    prob_grad = jnp.einsum(
        "sihd,sjhd->shij", grad_blocks, value_blocks, preferred_element_type=jnp.float32
    )
    value_back = jnp.einsum(
        "shij,sihd->sjhd", probs_low, grad_blocks, preferred_element_type=jnp.float32
    ).astype(jnp.bfloat16)
    centred = prob_grad - jnp.sum(probs * prob_grad, axis=3, keepdims=True)
    score_grad = (probs * centred * scale).astype(jnp.bfloat16)
    query_back = jnp.einsum(
        "shij,sjhd->sihd", score_grad, key_blocks, preferred_element_type=jnp.float32
    ).astype(jnp.bfloat16)
    key_back = jnp.einsum(
        "shij,sihd->sjhd", score_grad, query_blocks, preferred_element_type=jnp.float32
    ).astype(jnp.bfloat16)
    flat = (number * PATCHES, -1)
    return (query_back.reshape(flat), key_back.reshape(flat), value_back.reshape(flat))


def pinball_terms(estimate_entries, actual_entries):
    batch_example_tally = estimate_entries.shape[0]
    horizon_error = actual_entries[:, :, None] - estimate_entries.reshape(
        batch_example_tally, -1, LEVEL_CHANNELS
    )
    cumulative_share = jnp.arange(LEVEL_CHANNELS, dtype=jnp.float32) / LEVEL_CHANNELS
    mean_indicator = jnp.arange(LEVEL_CHANNELS) == 0
    lopsided_errors = jnp.where(
        mean_indicator,
        horizon_error * horizon_error,
        cumulative_share * horizon_error
        + SMOOTHING_RADIUS * jax.nn.softplus(-horizon_error / SMOOTHING_RADIUS),
    )
    skew_coefficient = (
        jnp.where(
            mean_indicator,
            -2.0 * horizon_error,
            jax.nn.sigmoid(-horizon_error / SMOOTHING_RADIUS) - cumulative_share,
        )
        / HORIZON_SPAN
    )
    return (
        jnp.sum(lopsided_errors) / HORIZON_SPAN,
        skew_coefficient.reshape(batch_example_tally, -1).astype(jnp.bfloat16),
    )


def multiplied_rows(left, right):

    def term(start, count):
        return jnp.dot(left, right, preferred_element_type=jnp.float32)

    return term


def per_device(
    history_sequences,
    later_steps,
    patch_lift_matrix,
    scaling_factors,
    asking_matrix,
    lookup_matrix,
    content_matrix,
    attend_exit_matrix,
    outlook_matrix,
):
    number = history_sequences.shape[0]
    rows_all = number * PATCHES
    patches, future_values = prepare(history_sequences, later_steps)
    embed_full, gains_full = (
        lax.all_gather(patch_lift_matrix, "dp", axis=1, tiled=True),
        lax.all_gather(scaling_factors, "dp", axis=1, tiled=True),
    )
    gains = gains_full.astype(jnp.float32)
    query_full, key_full, value_full, outlook_collected = (
        lax.all_gather(asking_matrix, "dp", axis=0, tiled=True),
        lax.all_gather(lookup_matrix, "dp", axis=0, tiled=True),
        lax.all_gather(content_matrix, "dp", axis=0, tiled=True),
        lax.all_gather(outlook_matrix, "dp", axis=0, tiled=True),
    )
    output_full = lax.all_gather(attend_exit_matrix, "dp", axis=1, tiled=True)
    residual_zero = jnp.dot(patches, embed_full, preferred_element_type=jnp.float32) + jnp.tile(
        positions(PATCHES, embed_full.shape[1]), (number, 1)
    )
    normed_attn, factor_attn = rms_forward(residual_zero, gains[0])
    queries = jnp.dot(normed_attn, query_full, preferred_element_type=jnp.float32).astype(
        jnp.bfloat16
    )
    keys = jnp.dot(normed_attn, key_full, preferred_element_type=jnp.float32).astype(jnp.bfloat16)
    values = jnp.dot(normed_attn, value_full, preferred_element_type=jnp.float32).astype(
        jnp.bfloat16
    )
    context, probs, probs_low = attention_forward(queries, keys, values, number)
    attn_term = multiplied_rows(context, output_full)
    residual_one = residual_zero + lax.psum(attn_term(0, rows_all), "mp")
    normed_head, factor_head = rms_forward(residual_one, gains[1])
    estimate_entries = jnp.dot(normed_head, outlook_collected, preferred_element_type=jnp.float32)
    device_portion = estimate_entries.shape[1] // LEVEL_CHANNELS
    actual_entries = lax.dynamic_slice_in_dim(
        future_values, lax.axis_index("mp") * device_portion, device_portion, 1
    )
    device_loss, estimate_derivative = pinball_terms(estimate_entries, actual_entries)
    total_loss_value = lax.psum(device_loss, ("dp", "mp"))
    loss_mean = total_loss_value / (number * PATCHES * lax.axis_size("dp"))
    head_weight_gradient = jnp.dot(
        normed_head.T, estimate_derivative, preferred_element_type=jnp.float32
    )
    head_contribution = multiplied_rows(estimate_derivative, outlook_collected.T)
    head_reverse = lax.psum(head_contribution(0, rows_all).astype(jnp.bfloat16), "mp").astype(
        jnp.float32
    )
    residual_one_grad, gain_one = rms_backward(residual_one, factor_head, gains[1], head_reverse)
    attn_low = residual_one_grad.astype(jnp.bfloat16)
    output_grad = jnp.dot(context.T, attn_low, preferred_element_type=jnp.float32)
    context_grad = jnp.dot(attn_low, output_full.T, preferred_element_type=jnp.float32).astype(
        jnp.bfloat16
    )
    query_back, key_back, value_back = attention_backward(
        context_grad, queries, keys, values, probs, probs_low, number
    )
    query_grad = jnp.dot(normed_attn.T, query_back, preferred_element_type=jnp.float32)
    key_grad = jnp.dot(normed_attn.T, key_back, preferred_element_type=jnp.float32)
    value_grad = jnp.dot(normed_attn.T, value_back, preferred_element_type=jnp.float32)
    total = jnp.dot(query_back, query_full.T, preferred_element_type=jnp.float32)
    total = total + jnp.dot(key_back, key_full.T, preferred_element_type=jnp.float32)
    attn_back = lax.psum(
        (total + jnp.dot(value_back, value_full.T, preferred_element_type=jnp.float32)).astype(
            jnp.bfloat16
        ),
        "mp",
    ).astype(jnp.float32)
    norm_back_zero, gain_zero = rms_backward(residual_zero, factor_attn, gains[0], attn_back)
    residual_zero_grad = residual_one_grad + norm_back_zero
    embed_grad = jnp.dot(
        patches.T, residual_zero_grad.astype(jnp.bfloat16), preferred_element_type=jnp.float32
    )
    gains_grad = jnp.stack([gain_zero, gain_one], axis=0)
    query_grad, key_grad, value_grad, head_weight_gradient = (
        lax.psum_scatter(query_grad, "dp", scatter_dimension=0, tiled=True),
        lax.psum_scatter(key_grad, "dp", scatter_dimension=0, tiled=True),
        lax.psum_scatter(value_grad, "dp", scatter_dimension=0, tiled=True),
        lax.psum_scatter(head_weight_gradient, "dp", scatter_dimension=0, tiled=True),
    )
    output_grad = lax.psum_scatter(output_grad, "dp", scatter_dimension=1, tiled=True)
    embed_grad, gains_grad = (
        lax.psum_scatter(embed_grad, "dp", scatter_dimension=1, tiled=True),
        lax.psum_scatter(gains_grad, "dp", scatter_dimension=1, tiled=True),
    )
    return (
        loss_mean,
        embed_grad,
        gains_grad,
        query_grad,
        key_grad,
        value_grad,
        output_grad,
        head_weight_gradient,
    )


def solution(mesh):
    in_specs = (
        P("dp", None),
        P("dp", None),
        P(None, "dp"),
        P(None, "dp"),
        P("dp", "mp"),
        P("dp", "mp"),
        P("dp", "mp"),
        P("mp", "dp"),
        P("dp", "mp"),
    )
    out_specs = (
        P(),
        P(None, "dp"),
        P(None, "dp"),
        P("dp", "mp"),
        P("dp", "mp"),
        P("dp", "mp"),
        P("mp", "dp"),
        P("dp", "mp"),
    )
    return jax.shard_map(
        per_device, mesh=mesh, in_specs=in_specs, out_specs=out_specs, check_vma=False
    )
```

profile of v0, /device:TPU:0, one launch (start us, length us, event | category | flops | bytes accessed | tf_op | source)
XLA Modules:
  0.0 517.2 jit_solution(183689326508854283)
XLA Ops:
  9.0 10.6 %all-gather.1 = bf16[8,160,2]{1,2,0:T(2,128)(2,1)S(1)} all-gather(bf16[1,160,2]{1,2,0:T(2,128)(2,1)} %bitcast.67), channel_id=1, replica_groups=mesh['dp'=8,'mp'=4] {'dp'}, dimensions={0}, use_global_device_ids=true | all-gather | bytes 5760 | tf_op jit(solution)/shard_map/all_gather | solution.py:157
  20.8 9.1 %all-gather = bf16[8,160,32]{1,2,0:T(8,128)(2,1)S(1)} all-gather(bf16[1,160,32]{1,2,0:T(8,128)(2,1)} %bitcast.66), channel_id=1, replica_groups=mesh['dp'=8,'mp'=4] {'dp'}, dimensions={0}, use_global_device_ids=true | all-gather | bytes 92160 | tf_op jit(solution)/shard_map/all_gather | solution.py:156
  30.5 10.3 %all_gather.24 = bf16[1280,320]{1,0:T(8,128)(2,1)S(1)} all-gather(bf16[160,320]{1,0:T(8,128)(2,1)S(1)} %copy-done.16), channel_id=1, replica_groups=mesh['dp'=8,'mp'=4] {'dp'}, dimensions={0}, use_global_device_ids=true | all-gather | bytes 921600 | tf_op jit(solution)/shard_map/all_gather | solution.py:161
  41.7 10.8 %all_gather.25 = bf16[1280,320]{1,0:T(8,128)(2,1)S(1)} all-gather(bf16[160,320]{1,0:T(8,128)(2,1)S(1)} %copy-done.17), channel_id=1, replica_groups=mesh['dp'=8,'mp'=4] {'dp'}, dimensions={0}, use_global_device_ids=true | all-gather | bytes 921600 | tf_op jit(solution)/shard_map/all_gather | solution.py:162
  54.2 10.2 %all_gather.23 = bf16[1280,320]{1,0:T(8,128)(2,1)S(1)} all-gather(bf16[160,320]{1,0:T(8,128)(2,1)S(1)} %copy-done.18), channel_id=1, replica_groups=mesh['dp'=8,'mp'=4] {'dp'}, dimensions={0}, use_global_device_ids=true | all-gather | bytes 921600 | tf_op jit(solution)/shard_map/all_gather | solution.py:163
  67.6 10.8 %all_gather.26 = bf16[320,1280]{0,1:T(8,128)(2,1)S(1)} all-gather(bf16[320,160]{0,1:T(8,128)(2,1)S(1)} %copy-done.19), channel_id=1, replica_groups=mesh['dp'=8,'mp'=4] {'dp'}, dimensions={1}, use_global_device_ids=true | all-gather | bytes 921600 | tf_op jit(solution)/shard_map/all_gather | solution.py:166
  81.5 11.6 %all_gather.27 = bf16[1280,320]{1,0:T(8,128)(2,1)} all-gather(bf16[160,320]{1,0:T(8,128)(2,1)S(1)} %copy-done.20), channel_id=1, replica_groups=mesh['dp'=8,'mp'=4] {'dp'}, dimensions={0}, use_global_device_ids=true | all-gather | bytes 921600 | tf_op jit(solution)/shard_map/all_gather | solution.py:164
  93.0 28.5 %all-reduce.4.cloned.1.call-done = f32[128,1280]{1,0:T(8,128)} async-done(((f32[128,1280]{1,0:T(8,128)}), f32[128,1280]{1,0:T(8,128)}) %all-reduce.4.cloned.1.call-update) | async-done | bytes 655376 | tf_op jit(solution)/shard_map/psum | solution.py:180
  127.1 35.1 %all-reduce.6.cloned.1.call-done = bf16[128,1280]{1,0:T(8,128)(2,1)} async-done(((bf16[128,1280]{1,0:T(8,128)(2,1)}), bf16[128,1280]{1,0:T(8,128)(2,1)}) %all-reduce.6.cloned.1.call-update) | async-done | bytes 327696 | tf_op jit(solution)/shard_map/psum | solution.py:194
  165.5 2.0 fusion.11
  167.7 2.0 fusion.9
  174.7 1.8 convolution_add_fusion.1
  177.8 36.1 %all-reduce.8.cloned.1.call-done = bf16[128,1280]{1,0:T(8,128)(2,1)} async-done(((bf16[128,1280]{1,0:T(8,128)(2,1)}), bf16[128,1280]{1,0:T(8,128)(2,1)}) %all-reduce.8.cloned.1.call-update) | async-done | bytes 327696 | tf_op jit(solution)/shard_map/psum | solution.py:211
  218.0 1.8 fusion.63
  220.0 1.8 fusion.71
  221.8 1.7 fusion.70
  225.4 1.8 fusion.68
  227.9 40.0 %psum.29 = f32[]{:T(128)} all-reduce(f32[]{:T(128)S(6)} %div.89), channel_id=1, replica_groups=mesh['dp'=8,'mp'=4] {'dp','mp'}, use_global_device_ids=true, to_apply=%region_7.8 | all-reduce | flops 1 | bytes 8 | tf_op jit(solution)/shard_map/psum | solution.py:188
  270.2 18.6 %reduce-scatter.22.cloned.1.call-done = f32[160,32]{1,0:T(8,128)} async-done(((f32[1280,32]{1,0:T(8,128)}), f32[160,32]{1,0:T(8,128)}) %reduce-scatter.22.cloned.1.call-update) | async-done | bytes 20496
  290.3 42.4 %reduce-scatter.20.cloned.1.call-done = f32[160,320]{1,0:T(8,128)} async-done(((f32[1280,320]{1,0:T(8,128)}), f32[160,320]{1,0:T(8,128)}) %reduce-scatter.20.cloned.1.call-update) | async-done | bytes 204816 | tf_op jit(solution)/shard_map/reduce_scatter | solution.py:227
  332.8 44.1 %reduce-scatter.18.cloned.1.call-done = f32[320,160]{0,1:T(8,128)} async-done(((f32[320,1280]{0,1:T(8,128)}), f32[320,160]{0,1:T(8,128)}) %reduce-scatter.18.cloned.1.call-update) | async-done | bytes 204816 | tf_op jit(solution)/shard_map/reduce_scatter | solution.py:229
  376.9 44.1 %reduce-scatter.16.cloned.1.call-done = f32[160,320]{1,0:T(8,128)} async-done(((f32[1280,320]{1,0:T(8,128)}), f32[160,320]{1,0:T(8,128)}) %reduce-scatter.16.cloned.1.call-update) | async-done | bytes 204816 | tf_op jit(solution)/shard_map/reduce_scatter | solution.py:226
  421.0 44.1 %reduce-scatter.14.cloned.1.call-done = f32[160,320]{1,0:T(8,128)} async-done(((f32[1280,320]{1,0:T(8,128)}), f32[160,320]{1,0:T(8,128)}) %reduce-scatter.14.cloned.1.call-update) | async-done | bytes 204816 | tf_op jit(solution)/shard_map/reduce_scatter | solution.py:225
  465.2 44.0 %reduce-scatter.12.cloned.1.call-done = f32[160,320]{1,0:T(8,128)} async-done(((f32[1280,320]{1,0:T(8,128)}), f32[160,320]{1,0:T(8,128)}) %reduce-scatter.12.cloned.1.call-update) | async-done | bytes 204816 | tf_op jit(solution)/shard_map/reduce_scatter | solution.py:224
  (148 shorter events, 36.7 us)
Async XLA Ops:
  7.2 23.3 %copy-start.16 = (bf16[160,320]{1,0:T(8,128)(2,1)S(1)}, bf16[160,320]{1,0:T(8,128)(2,1)}, u32[]{:S(2)}) copy-start(bf16[160,320]{1,0:T(8,128)(2,1)} %param.13) | copy-start | bytes 307204
  7.2 114.4 %all-reduce.4.cloned.1.call-start = ((), (), s32[]{:S(2)}) async-start(), calls=%async_computation.7 | async-start | bytes 1310720 | tf_op jit(solution)/shard_map/psum | solution.py:180
  30.4 11.2 %copy-start.17 = (bf16[160,320]{1,0:T(8,128)(2,1)S(1)}, bf16[160,320]{1,0:T(8,128)(2,1)}, u32[]{:S(2)}) copy-start(bf16[160,320]{1,0:T(8,128)(2,1)} %param.14) | copy-start | bytes 307204
  41.4 12.8 %copy-start.18 = (bf16[160,320]{1,0:T(8,128)(2,1)S(1)}, bf16[160,320]{1,0:T(8,128)(2,1)}, u32[]{:S(2)}) copy-start(bf16[160,320]{1,0:T(8,128)(2,1)} %param.15) | copy-start | bytes 307204
  41.7 24.5 %copy-start.14 = (bf16[8,16,4,80]{3,2,1,0:T(4,128)(2,1)}, bf16[8,16,4,80]{3,2,1,0:T(4,128)(2,1)S(1)}, u32[]{:S(2)}) copy-start(bf16[8,16,4,80]{3,2,1,0:T(4,128)(2,1)S(1)} %reshape.114) | copy-start | bytes 245764
  54.2 13.1 %copy-start.15 = (bf16[8,16,4,80]{3,2,1,0:T(4,128)(2,1)}, bf16[8,16,4,80]{3,2,1,0:T(4,128)(2,1)S(1)}, u32[]{:S(2)}) copy-start(bf16[8,16,4,80]{3,2,1,0:T(4,128)(2,1)S(1)} %reshape.115) | copy-start | bytes 245764
  65.4 2.2 copy-start.19
  67.3 13.3 %copy-start.21 = (f32[8,128]{1,0:T(8,128)S(1)}, f32[8,128]{1,0:T(8,128)}, u32[]{:S(2)}) copy-start(f32[8,128]{1,0:T(8,128)} %param.10) | copy-start | bytes 12292
  67.6 13.3 %copy-start.7 = (bf16[128,320]{1,0:T(8,128)(2,1)}, bf16[128,320]{1,0:T(8,128)(2,1)S(1)}, u32[]{:S(2)}) copy-start(bf16[128,320]{1,0:T(8,128)(2,1)S(1)} %reshape.116) | copy-start | bytes 245764
  80.6 81.6 %all-reduce.6.cloned.1.call-start = ((), (), s32[]{:S(2)}) async-start(), calls=%async_computation.8 | async-start | bytes 655360 | tf_op jit(solution)/shard_map/psum | solution.py:194
  123.0 3.4 copy-start.23
  126.1 87.8 %all-reduce.8.cloned.1.call-start = ((), (), s32[]{:S(2)}) async-start(), calls=%async_computation.9 | async-start | bytes 655360 | tf_op jit(solution)/shard_map/psum | solution.py:211
  162.2 2.5 copy-start.4
  172.3 2.5 copy-start.9
  173.5 3.0 copy-start.2
  176.6 39.9 %copy-start.6 = (bf16[128,1280]{1,0:T(8,128)(2,1)S(1)}, bf16[128,1280]{1,0:T(8,128)(2,1)}, u32[]{:S(2)}) copy-start(bf16[128,1280]{1,0:T(8,128)(2,1)} %all-reduce.6.cloned.1.call-done) | copy-start | bytes 983044
  177.7 90.9 %reduce-scatter.24.cloned.1.call-start = ((), (), s32[]{:S(2)}) async-start(), calls=%async_computation.16 | async-start | bytes 737280
  213.9 2.5 copy-start.13
  216.4 72.4 %reduce-scatter.22.cloned.1.call-start = ((), (), s32[]{:S(2)}) async-start(), calls=%async_computation.15 | async-start | bytes 737280
  218.0 114.8 %reduce-scatter.20.cloned.1.call-start = ((), (), s32[]{:S(2)}) async-start(), calls=%async_computation.14 | async-start | bytes 2211840 | tf_op jit(solution)/shard_map/reduce_scatter | solution.py:227
  219.9 157.0 %reduce-scatter.18.cloned.1.call-start = ((), (), s32[]{:S(2)}) async-start(), calls=%async_computation.13 | async-start | bytes 2211840 | tf_op jit(solution)/shard_map/reduce_scatter | solution.py:229
  221.7 199.3 %reduce-scatter.16.cloned.1.call-start = ((), (), s32[]{:S(2)}) async-start(), calls=%async_computation.12 | async-start | bytes 2211840 | tf_op jit(solution)/shard_map/reduce_scatter | solution.py:226
  223.6 241.6 %reduce-scatter.14.cloned.1.call-start = ((), (), s32[]{:S(2)}) async-start(), calls=%async_computation.11 | async-start | bytes 2211840 | tf_op jit(solution)/shard_map/reduce_scatter | solution.py:225
  225.4 283.8 %reduce-scatter.12.cloned.1.call-start = ((), (), s32[]{:S(2)}) async-start(), calls=%async_computation.10 | async-start | bytes 2211840 | tf_op jit(solution)/shard_map/reduce_scatter | solution.py:224
  (10 other events, 13.4 us)
Sparse Core Ops, SparseCore 0:
  80.7 40.7 all-reduce.3
  126.2 35.9 all-reduce.5
  177.9 36.0 all-reduce.7
  216.9 34.3 reduce-scatter.23
  254.3 34.4 reduce-scatter.21
  292.6 40.1 reduce-scatter.19
  336.7 40.1 reduce-scatter.17
  380.9 40.1 reduce-scatter.15
  425.0 40.1 reduce-scatter.13
  469.0 40.1 reduce-scatter.11
where the time goes:
time: 518 us; the launch traced here: 517 us
  waiting for transfers between devices  337 us (65%)
  blocking collectives  113 us (22%)
  matrix products  26.5 us (5%)
  between operations  17.2 us (3%)
  local copies, waits for them, and re-layouts  13.3 us (3%)
  other arithmetic  8.96 us (2%)
    reduce_scatter x1, waiting for transfers between devices, per_device(): lax.psum_scatter(key_grad, 'dp', scatter_dimension=0, tiled=True)  44.1 us
    reduce_scatter x1, waiting for transfers between devices, per_device(): lax.psum_scatter(output_grad, 'dp', scatter_dimension=1, tiled=True)  44.1 us
    reduce_scatter x1, waiting for transfers between devices, per_device(): lax.psum_scatter(value_grad, 'dp', scatter_dimension=0, tiled=True)  44.1 us
    reduce_scatter x1, waiting for transfers between devices, per_device(): lax.psum_scatter(query_grad, 'dp', scatter_dimension=0, tiled=True)  44 us
    reduce_scatter x1, waiting for transfers between devices, per_device(): lax.psum_scatter(head_weight_gradient, 'dp', scatter_dimension=0, tiled=T...  42.4 us
    psum x1, blocking collectives, per_device(): total_loss_value = lax.psum(device_loss, ('dp', 'mp'))  40 us
    psum x1, waiting for transfers between devices, per_device(): lax.psum((total + jnp.dot(value_back, value_full.T, preferred_element_typ...  36.1 us
    psum x1, waiting for transfers between devices, per_device(): lax.psum(head_contribution(0, rows_all).astype(jnp.bfloat16), 'mp')  35.1 us
  transfers between devices with their start and end apart: 10, of which 9 were waited for; matrix products, arithmetic and copies ran while one was open for 3% of the time, Pallas kernels for 0%

commit v1 on v0

--- a/solution.py
+++ b/solution.py
@@ -1,8 +1,12 @@
+import functools
 import math
 
 import jax
 import jax.numpy as jnp
+import numpy as np
 from jax import lax
+from jax.experimental import pallas as pl
+from jax.experimental.pallas import tpu as pltpu
 from jax.sharding import PartitionSpec as P
 
 PATCH = 32
@@ -243,6 +247,549 @@
     )
 
 
+MESH = pl.DeviceIdType.MESH
+BF = jnp.bfloat16
+F32 = jnp.float32
+
+
+def mm(left, right, dims=(1, 0)):
+    return lax.dot_general(
+        left, right, (((dims[0],), (dims[1],)), ((), ())), preferred_element_type=F32
+    )
+
+
+def position_table(length, width):
+    half = width // 2
+    freqs = np.exp(-math.log(10000.0) * np.arange(half, dtype=np.float32) / np.float32(half))
+    angles = np.arange(length, dtype=np.float32)[:, None] * freqs.astype(np.float32)[None, :]
+    return np.concatenate([np.sin(angles), np.cos(angles)], axis=1).astype(np.float32)
+
+
+EG, WQ, WK, WV, WO, WH, CTX, FG, QB, KB, VB = range(11)
+NA, NH, AL, EP = range(4)
+
+
+def sublayer_kernel(
+    sizes,
+    hist,
+    later,
+    eg_in,
+    wq_in,
+    wk_in,
+    wv_in,
+    wo_in,
+    wh_in,
+    pos,
+    share,
+    loss_out,
+    eg_out,
+    q_out,
+    k_out,
+    v_out,
+    o_out,
+    h_out,
+    eg_full,
+    wq_full,
+    wk_full,
+    wv_full,
+    wo_full,
+    wh_full,
+    ctx_full,
+    fg_full,
+    qb_full,
+    kb_full,
+    vb_full,
+    turned,
+    na_all,
+    nh_all,
+    al_all,
+    ep_all,
+    parts,
+    parts_in,
+    nh_full,
+    al_full,
+    rz_ref,
+    patch_ref,
+    probs_ref,
+    egz_own,
+    egz_all,
+    loss_own,
+    loss_dp,
+    loss_mid,
+    loss_mp,
+    ag_send,
+    ag_recv,
+    xx_send,
+    xx_recv,
+    z_send,
+    z_recv,
+    l_send,
+    l_recv,
+):
+    dp, mp = sizes
+    chips = dp // 2
+    me = lax.axis_index("dp")
+    mz = lax.axis_index("mp")
+    core = lax.rem(me, 2)
+    chip = me // 2
+    twin = chip * 2 + 1 - core
+    number, steps = hist.shape
+    rows = number * PATCHES
+    width = pos.shape[1]
+    cut = width // dp
+    shard = rows // mp
+    cols = wq_in.shape[1]
+    heads = cols // HEAD_DIM
+
+    def rotated(k):
+        return lax.rem(me + k, dp)
+
+    def chip_at(k):
+        return lax.rem(chip + k + chips, chips) * 2 + core
+
+    barrier = pltpu.get_barrier_semaphore()
+    for k in range(1, dp):
+        pl.semaphore_signal(barrier, inc=1, device_id=(rotated(k), mz), device_id_type=MESH)
+    for k in range(1, mp):
+        pl.semaphore_signal(
+            barrier, inc=1, device_id=(me, lax.rem(mz + k, mp)), device_id_type=MESH
+        )
+    pl.semaphore_wait(barrier, dp - 1 + mp - 1)
+
+    fulls = [
+        eg_full, wq_full, wk_full, wv_full, wo_full, wh_full,
+        ctx_full, fg_full, qb_full, kb_full, vb_full,
+    ]
+
+    def block(full, owner):
+        size = full.shape[0] // dp
+        return full.at[pl.ds(pl.multiple_of(owner * size, 16), size), :]
+
+    def remote(src, dst, send, recv, device):
+        return pltpu.make_async_remote_copy(
+            src_ref=src, dst_ref=dst, send_sem=send, recv_sem=recv,
+            device_id=device, device_id_type=MESH,
+        )
+
+    def ag_copy(i, slot, owner, target, src=None):
+        place = block(fulls[i], owner)
+        return remote(
+            place if src is None else src, place,
+            ag_send.at[i, slot], ag_recv.at[i, slot], (target, mz),
+        )
+
+    def ag_start(i, src=None):
+        for k in range(1, chips):
+            ag_copy(i, k, me, chip_at(k), src).start()
+        ag_copy(i, 0, me, twin, src).start()
+
+    def ag_finish(i):
+        for k in range(1, chips):
+            owner = chip_at(-k)
+            ag_copy(i, k, owner, twin).wait_recv()
+            ag_copy(i, chips - 1 + k, owner, twin).start()
+        ag_copy(i, 0, twin, twin).wait_recv()
+        for k in range(1, chips):
+            other = lax.rem(chip - k + chips, chips) * 2 + 1 - core
+            ag_copy(i, chips - 1 + k, other, twin).wait_recv()
+
+    def ag_drain(i, src=None):
+        for k in range(1, chips):
+            ag_copy(i, k, me, chip_at(k), src).wait_send()
+            ag_copy(i, chips - 1 + k, chip_at(-k), twin).wait_send()
+        ag_copy(i, 0, me, twin, src).wait_send()
+
+    def store_own(i, value):
+        size = fulls[i].shape[0] // dp
+        fulls[i][pl.ds(pl.multiple_of(me * size, 16), size), :] = value
+
+    lands = [na_all, nh_all, al_all, ep_all]
+
+    def xx_copy(i, k, sender, target):
+        if i == EP:
+            dst = ep_all.at[sender]
+        else:
+            dst = lands[i].at[:, pl.ds(pl.multiple_of(sender * rows, 128), rows)]
+        return remote(
+            turned.at[i, pl.ds(pl.multiple_of(target * cut, 16), cut), :], dst,
+            xx_send.at[i, k], xx_recv.at[i, k], (target, mz),
+        )
+
+    def xx_start(i, value):
+        turned[i] = value
+        for k in range(1, dp):
+            xx_copy(i, k, me, rotated(k)).start()
+        own = turned[i, pl.ds(pl.multiple_of(me * cut, 16), cut), :]
+        if i == EP:
+            ep_all[me] = own
+        else:
+            lands[i][:, pl.ds(pl.multiple_of(me * rows, 128), rows)] = own
+
+    def xx_finish(i):
+        for k in range(1, dp):
+            xx_copy(i, k, lax.rem(me - k + dp, dp), rotated(k)).wait_recv()
+
+    def xx_drain(i):
+        for k in range(1, dp):
+            xx_copy(i, k, me, rotated(k)).wait_send()
+
+    def z_at(k):
+        return lax.rem(mz + k + mp, mp)
+
+    def rs_copy(i, k, sender, target):
+        return remote(
+            parts.at[i, pl.ds(pl.multiple_of(target * shard, 16), shard), :],
+            parts_in.at[i, sender],
+            z_send.at[i, k], z_recv.at[i, k], (me, target),
+        )
+
+    def rs_start(i, value):
+        parts[i] = value.astype(BF)
+        for k in range(1, mp):
+            rs_copy(i, k, mz, z_at(k)).start()
+
+    def rs_finish(i):
+        total = parts[i, pl.ds(pl.multiple_of(mz * shard, 16), shard), :].astype(F32)
+        for k in range(1, mp):
+            rs_copy(i, k, z_at(-k), z_at(k)).wait_recv()
+            total = total + parts_in[i, z_at(-k)].astype(F32)
+        return total
+
+    def zg_copy(i, full, k, owner):
+        place = full.at[pl.ds(pl.multiple_of(owner * shard, 16), shard), :]
+        return remote(place, place, z_send.at[i, k], z_recv.at[i, k], (me, z_at(k)))
+
+    def zg(i, full, value):
+        full[pl.ds(pl.multiple_of(mz * shard, 16), shard), :] = value
+        for k in range(1, mp):
+            zg_copy(i, full, k, mz).start()
+
+    def zg_finish(i, full):
+        for k in range(1, mp):
+            zg_copy(i, full, k, z_at(-k)).wait_recv()
+
+    inputs = [eg_in, wq_in, wk_in, wv_in, wo_in, wh_in]
+    for i, ref in enumerate(inputs):
+        ag_start(i, ref)
+    for i, ref in enumerate(inputs):
+        store_own(i, ref[...])
+
+    history = hist[...]
+    centre = jnp.mean(history, axis=1, keepdims=True)
+    spread = jnp.sqrt(
+        jnp.mean((history - centre) * (history - centre), axis=1, keepdims=True) + STAT_EPS
+    )
+    normed = (history - centre) / spread
+    ahead = (later[...] - centre) / spread
+    joined = jnp.concatenate([normed, ahead], axis=1)
+    span = joined.shape[1]
+    wide = jnp.broadcast_to(joined[:, None, :], (number, PATCHES, span)).reshape(rows, span)
+    row = lax.broadcasted_iota(jnp.int32, (rows, span), 0)
+    at = lax.broadcasted_iota(jnp.int32, (rows, span), 1)
+    offset = at - PATCH * (row & (PATCHES - 1))
+    here = (offset >= 0) & (offset < PATCH)
+    lane = lax.broadcasted_iota(jnp.int32, (span, 128), 1)
+    low = lax.broadcasted_iota(jnp.int32, (span, 128), 0) & (PATCH - 1)
+    fold = jnp.where(lane == low, 1.0, 0.0).astype(BF)
+    patches = mm(jnp.where(here, wide, 0.0).astype(BF), fold).astype(BF)
+    patch_ref[...] = patches
+
+    portion = cols // LEVEL_CHANNELS
+    reach = offset - PATCH - portion * mz
+    chosen = jnp.where((reach >= 0) & (reach < portion), wide, 0.0)
+    column = lax.broadcasted_iota(jnp.int32, (span, cols), 1)
+    first = (lax.broadcasted_iota(jnp.int32, (span, cols), 0) & (PATCH - 1)) * LEVEL_CHANNELS
+    spreader = jnp.where((column >= first) & (column < first + LEVEL_CHANNELS), 1.0, 0.0).astype(BF)
+    target = jnp.zeros((rows, cols), F32)
+    rest = chosen
+    for _ in range(3):
+        piece = rest.astype(BF)
+        target = target + mm(piece, spreader)
+        rest = rest - piece.astype(F32)
+
+    ag_finish(EG)
+    lifted = eg_full[...]
+    table = jnp.broadcast_to(pos[...][None], (number, PATCHES, width)).reshape(rows, width)
+    rz = mm(patches, lifted, (1, 1)) + table
+    rz_ref[...] = rz
+    pick = lax.broadcasted_iota(jnp.int32, (16, 128), 1) - lax.broadcasted_iota(
+        jnp.int32, (16, 128), 0
+    )
+    gains = mm(jnp.where(pick == PATCH, 1.0, 0.0).astype(BF), lifted, (1, 1))
+    gain_attn = gains[0:1, :]
+    gain_head = gains[1:2, :]
+    factor = lax.rsqrt(jnp.mean(rz * rz, axis=1, keepdims=True) + EPS)
+    na = rz * factor * gain_attn
+    na_low = na.astype(BF)
+    xx_start(NA, na.T.astype(BF))
+
+    ag_finish(WQ)
+    q = mm(na_low, wq_full[...])
+    ag_finish(WK)
+    k_ = mm(na_low, wk_full[...])
+    ag_finish(WV)
+    v = mm(na_low, wv_full[...])
+    q_low, k_low, v_low = q.astype(BF), k_.astype(BF), v.astype(BF)
+
+    head_lane = lax.broadcasted_iota(jnp.int32, (1, cols), 1)
+    masks = [
+        jnp.where((head_lane >= h * HEAD_DIM) & (head_lane < (h + 1) * HEAD_DIM), 1.0, 0.0)
+        for h in range(heads)
+    ]
+    r_at = lax.broadcasted_iota(jnp.int32, (rows, rows), 0)
+    c_at = lax.broadcasted_iota(jnp.int32, (rows, rows), 1)
+    causal = (c_at <= r_at) & (c_at >= r_at - (r_at & (PATCHES - 1)))
+    scale = 1.0 / math.sqrt(HEAD_DIM)
+    ctx = jnp.zeros((rows, cols), F32)
+    for h in range(heads):
+        scores = mm((q * masks[h]).astype(BF), k_low, (1, 1)) * scale
+        raised = jnp.where(causal, jnp.exp(scores), 0.0)
+        probs = raised / jnp.sum(raised, axis=1, keepdims=True)
+        probs_ref[h] = probs
+        ctx = ctx + mm(probs.astype(BF), (v * masks[h]).astype(BF))
+    ctx_low = ctx.astype(BF)
+    store_own(CTX, ctx_low)
+    ag_start(CTX)
+    ag_finish(WO)
+    rs_start(0, mm(ctx_low, wo_full[...], (1, 1)))
+    ag_finish(WH)
+    shard_rows = pl.ds(pl.multiple_of(mz * shard, 16), shard)
+    rz_shard = rz_ref[shard_rows, :]
+    r1 = rz_shard + rs_finish(0)
+    factor_head = lax.rsqrt(jnp.mean(r1 * r1, axis=1, keepdims=True) + EPS)
+    zg(3, nh_full, (r1 * factor_head * gain_head).astype(BF))
+    zg_finish(3, nh_full)
+    nh = nh_full[...]
+    error = target - mm(nh, wh_full[...])
+    shares = share[0:1, :]
+    is_mean = shares == 0.0
+    slope = -error / SMOOTHING_RADIUS
+    small = jnp.exp(-jnp.abs(slope))
+    soft = jnp.maximum(slope, 0.0) + jnp.log1p(small)
+    sig = jnp.where(slope >= 0.0, 1.0, small) / (1.0 + small)
+    terms = jnp.where(is_mean, error * error, shares * error + SMOOTHING_RADIUS * soft)
+    fg = (jnp.where(is_mean, -2.0 * error, sig - shares) / HORIZON_SPAN).astype(BF)
+    store_own(FG, fg)
+    ag_start(FG)
+    rs_start(1, mm(fg, wh_full[...], (1, 1)))
+    xx_start(NH, nh.astype(F32).T.astype(BF))
+    loss_here = jnp.sum(jnp.sum(terms, axis=1, keepdims=True), axis=0, keepdims=True)
+    loss_own[...] = jnp.broadcast_to(loss_here, loss_own.shape)
+
+    def loss_copy(k, sender):
+        return remote(
+            loss_own, loss_dp.at[sender], l_send.at[0, k], l_recv.at[0, k], (rotated(k), mz)
+        )
+
+    def loss_z(k, sender):
+        return remote(
+            loss_mid, loss_mp.at[sender], l_send.at[1, k], l_recv.at[1, k], (me, z_at(k))
+        )
+
+    for k in range(1, dp):
+        loss_copy(k, me).start()
+    ag_finish(CTX)
+
+    up = rs_finish(1)
+    weighted = gain_head * up
+    inner = jnp.mean(weighted * r1, axis=1, keepdims=True)
+    r1_grad = factor_head * weighted - r1 * factor_head * factor_head * factor_head * inner
+    gain_one = jnp.sum(up * r1 * factor_head, axis=0, keepdims=True)
+    zg(4, al_full, r1_grad.astype(BF))
+    ag_finish(FG)
+    zg_finish(4, al_full)
+    al = al_full[...]
+    cg = mm(al, wo_full[...])
+    qb = jnp.zeros((rows, cols), F32)
+    kb = jnp.zeros((rows, cols), F32)
+    vb = jnp.zeros((rows, cols), F32)
+    for h in range(heads):
+        cg_head = (cg * masks[h]).astype(BF)
+        probs = probs_ref[h]
+        prob_grad = mm(cg_head, v_low, (1, 1))
+        vb = vb + mm(probs.T.astype(BF), cg_head)
+        centred = prob_grad - jnp.sum(probs * prob_grad, axis=1, keepdims=True)
+        score_grad = probs * centred * scale
+        qb = qb + mm(score_grad.astype(BF), (k_ * masks[h]).astype(BF))
+        kb = kb + mm(score_grad.T.astype(BF), (q * masks[h]).astype(BF))
+    qb, kb, vb = qb.astype(BF), kb.astype(BF), vb.astype(BF)
+    for i, value in ((QB, qb), (KB, kb), (VB, vb)):
+        store_own(i, value)
+        ag_start(i)
+    back = mm(qb, wq_full[...], (1, 1)) + mm(kb, wk_full[...], (1, 1))
+    rs_start(2, back + mm(vb, wv_full[...], (1, 1)))
+    xx_start(AL, al.astype(F32).T.astype(BF))
+
+    total = loss_own[...]
+    for k in range(1, dp):
+        loss_copy(k, lax.rem(me - k + dp, dp)).wait_recv()
+        total = total + loss_dp[lax.rem(me - k + dp, dp)]
+    loss_mid[...] = total
+    for k in range(1, mp):
+        loss_z(k, mz).start()
+    xx_finish(NH)
+    h_out[...] = mm(nh_all[...], fg_full[...])
+
+    up = rs_finish(2)
+    factor = lax.rsqrt(jnp.mean(rz_shard * rz_shard, axis=1, keepdims=True) + EPS)
+    weighted = gain_attn * up
+    inner = jnp.mean(weighted * rz_shard, axis=1, keepdims=True)
+    rz_grad = r1_grad + (factor * weighted - rz_shard * factor * factor * factor * inner)
+    gain_zero = jnp.sum(up * rz_shard * factor, axis=0, keepdims=True)
+    which = lax.broadcasted_iota(jnp.int32, (16, width), 0)
+    both = jnp.where(which == 0, gain_zero, jnp.where(which == 1, gain_one, 0.0))
+    both_high = both.astype(BF).astype(F32)
+    stacked = jnp.concatenate([rz_grad, both_high, both - both_high], axis=0)
+    hot = jnp.where(pick == PATCH, 1.0, 0.0)
+    other = jnp.concatenate([patch_ref[shard_rows, :].astype(F32), hot, hot], axis=0)
+    xx_start(EP, mm(stacked.T.astype(BF), other.astype(BF)).astype(BF))
+
+    total = loss_mid[...]
+    for k in range(1, mp):
+        loss_z(k, z_at(-k)).wait_recv()
+        total = total + loss_mp[z_at(-k)]
+    loss_out[...] = total / (number * PATCHES * dp * HORIZON_SPAN)
+    for i in (QB, KB, VB):
+        ag_finish(i)
+
+    xx_finish(EP)
+    summed = ep_all[0].astype(F32)
+    for d in range(1, dp):
+        summed = summed + ep_all[d].astype(F32)
+    egz_own[...] = summed.astype(BF)
+
+    def egz(k, sender):
+        return remote(egz_own, egz_all.at[sender], z_send.at[5, k], z_recv.at[5, k], (me, z_at(k)))
+
+    for k in range(1, mp):
+        egz(k, mz).start()
+
+    xx_finish(NA)
+    na_every = na_all[...]
+    q_out[...] = mm(na_every, qb_full[...])
+    k_out[...] = mm(na_every, kb_full[...])
+    v_out[...] = mm(na_every, vb_full[...])
+    xx_finish(AL)
+    o_out[...] = mm(al_all[...], ctx_full[...])
+    for k in range(1, mp):
+        egz(k, z_at(-k)).wait_recv()
+        summed = summed + egz_all[z_at(-k)].astype(F32)
+    eg_out[...] = summed
+
+    for i in range(len(fulls)):
+        ag_drain(i, inputs[i] if i < len(inputs) else None)
+    for i in range(4):
+        xx_drain(i)
+    for k in range(1, dp):
+        loss_copy(k, me).wait_send()
+    for k in range(1, mp):
+        for i in range(3):
+            rs_copy(i, k, mz, z_at(k)).wait_send()
+        zg_copy(3, nh_full, k, mz).wait_send()
+        zg_copy(4, al_full, k, mz).wait_send()
+        egz(k, mz).wait_send()
+        loss_z(k, mz).wait_send()
+
+
+def fused_device(
+    dp,
+    mp,
+    history_sequences,
+    later_steps,
+    patch_lift_matrix,
+    scaling_factors,
+    asking_matrix,
+    lookup_matrix,
+    content_matrix,
+    attend_exit_matrix,
+    outlook_matrix,
+):
+    number = history_sequences.shape[0]
+    rows = number * PATCHES
+    cut, cols = asking_matrix.shape
+    width = cut * dp
+    small = jnp.concatenate([patch_lift_matrix, scaling_factors], axis=0)
+    small = jnp.pad(small, ((0, 128 - small.shape[0]), (0, 0))).T
+    levels = np.arange(cols) % LEVEL_CHANNELS
+    share = np.broadcast_to((levels.astype(np.float32) / LEVEL_CHANNELS)[None], (8, cols))
+    vmem = pltpu.VMEM
+    full = vmem((width, cols), BF)
+    tall = vmem((rows * dp, cols), BF)
+    across = vmem((cut, rows * dp), BF)
+    dma = pltpu.SemaphoreType.DMA
+    grad = jax.ShapeDtypeStruct((cut, cols), F32)
+    shard = rows // mp
+    chips = dp // 2
+    loss, small_grad, query_grad, key_grad, value_grad, output_grad, head_grad = pl.pallas_call(
+        functools.partial(sublayer_kernel, (dp, mp)),
+        out_shape=(
+            jax.ShapeDtypeStruct((8, 128), F32),
+            jax.ShapeDtypeStruct((cut, 128), F32),
+            grad, grad, grad, grad, grad,
+        ),
+        in_specs=[pl.BlockSpec(memory_space=vmem)] * 10,
+        out_specs=(pl.BlockSpec(memory_space=vmem),) * 7,
+        scratch_shapes=[
+            vmem((width, 128), BF), full, full, full, full, full,
+            tall, tall, tall, tall, tall,
+            vmem((4, width, rows), BF),
+            across, across, across,
+            vmem((dp, cut, rows), BF),
+            vmem((3, rows, width), BF),
+            vmem((3, mp, shard, width), BF),
+            vmem((rows, width), BF),
+            vmem((rows, width), BF),
+            vmem((rows, width), F32),
+            vmem((rows, 128), BF),
+            vmem((cols // HEAD_DIM, rows, rows), F32),
+            vmem((cut, 128), BF),
+            vmem((mp, cut, 128), BF),
+            vmem((8, 128), F32),
+            vmem((dp, 8, 128), F32),
+            vmem((8, 128), F32),
+            vmem((mp, 8, 128), F32),
+            dma((11, 2 * chips - 1)), dma((11, 2 * chips - 1)),
+            dma((4, dp)), dma((4, dp)),
+            dma((6, mp)), dma((6, mp)),
+            dma((2, max(dp, mp))), dma((2, max(dp, mp))),
+        ],
+        compiler_params=pltpu.CompilerParams(
+            collective_id=0, has_side_effects=True, vmem_limit_bytes=56 * 1024 * 1024
+        ),
+    )(
+        history_sequences, later_steps, small, asking_matrix, lookup_matrix, content_matrix,
+        attend_exit_matrix.T, outlook_matrix,
+        jnp.asarray(position_table(PATCHES, width)), jnp.asarray(share),
+    )
+    lift = patch_lift_matrix.shape[0]
+    gains = scaling_factors.shape[0]
+    return (
+        loss[0, 0],
+        small_grad[:, :lift].T,
+        small_grad[:, lift : lift + gains].T,
+        query_grad,
+        key_grad,
+        value_grad,
+        output_grad.T,
+        head_grad,
+    )
+
+
+def fits(dp, mp, arrays):
+    rows = arrays[0].shape[0] * PATCHES
+    cut, cols = arrays[4].shape
+    return (
+        rows == 128
+        and dp % 2 == 0
+        and dp > 2
+        and mp > 1
+        and cut % 16 == 0
+        and rows % (16 * mp) == 0
+        and cols % HEAD_DIM == 0
+        and cols == PATCH * LEVEL_CHANNELS
+    )
+
+
 def solution(mesh):
     in_specs = (
         P("dp", None),
@@ -265,6 +812,13 @@
         P("mp", "dp"),
         P("dp", "mp"),
     )
+    dp, mp = mesh.shape["dp"], mesh.shape["mp"]
+
+    def step(*arrays):
+        if fits(dp, mp, arrays):
+            return fused_device(dp, mp, *arrays)
+        return per_device(*arrays)
+
     return jax.shard_map(
-        per_device, mesh=mesh, in_specs=in_specs, out_specs=out_specs, check_vma=False
-    )
+        step, mesh=mesh, in_specs=in_specs, out_specs=out_specs, check_vma=False
+    )

time: 518 us -> 111 us (0.21)
  waiting for transfers between devices: 337 us -> 0 us
  blocking collectives: 113 us -> 0 us
  Pallas kernels: 0 us -> 99.3 us
  matrix products: 26.5 us -> 0 us
  between operations: 17.2 us -> 0.7 us
  other arithmetic: 8.96 us -> 0.71 us
    reduce_scatter x5 -> x0, waiting for transfers between devices: 219 us -> none  [the longest x1 44.1 us: per_device(): lax.psum_scatter(key_grad, 'dp', scatter_dimension=0, tiled=True)]
    psum x3 -> x0, waiting for transfers between devices: 99.7 us -> none  [the longest x1 36.1 us: per_device(): lax.psum((total + jnp.dot(value_back, value_full.T, preferred_element_typ...]
    pallas_call x0 -> x1, Pallas kernels: none -> 99.3 us  [fused_device(): pl.pallas_call(functools.partial(sublayer_kernel, (dp, mp)), out_shape=(j...]
    all_gather x7 -> x0, blocking collectives: 73.2 us -> none  [the longest x1 11.6 us: per_device(): lax.all_gather(outlook_matrix, 'dp', axis=0, tiled=True)]
    psum x1 -> x0, blocking collectives: 40 us -> none  [per_device(): total_loss_value = lax.psum(device_loss, ('dp', 'mp'))]
    dot_general x22 -> x0, matrix products: 25 us -> none  [the longest x2 2.57 us: term(): return jnp.dot(left, right, preferred_element_type=jnp.float32)]
    unnamed x12 -> x0, waiting for transfers between devices: 18.8 us -> none
    reduce_sum x5 -> x0, other arithmetic: 5.61 us -> none  [the longest x2 2.54 us: rms_backward(): gain_term = jnp.sum(upstream * residual * factor, axis=0)]
  transfers between devices with their start and end apart: 10 -> 0, of which waited for: 9 -> 0; matrix products, arithmetic and copies ran while one was open for 3% -> 0% of each run, Pallas kernels for 0% -> 0%
where the time goes in v1:
time: 111 us
  Pallas kernels  99.3 us (89%)
  local copies, waits for them, and re-layouts  10.1 us (9%)
    pallas_call x1, Pallas kernels, fused_device(): pl.pallas_call(functools.partial(sublayer_kernel, (dp, mp)), out_shape=(j...  99.3 us
    unnamed x25, local copies, waits for them, and re-layouts  7.38 us

profile of v1, /device:TPU:0, one launch (start us, length us, event | category | flops | bytes accessed | tf_op | source)
XLA Modules:
  0.0 110.8 jit_solution(2568470996843841734)
XLA Ops:
  0.6 0.0 copy-start.7
  0.6 0.8 copy.19
  1.5 0.0 copy-done.7
  1.5 0.1 copy.20
  1.6 0.0 copy-start.6
  1.6 0.7 fusion.3.eg_in
  2.3 0.0 copy-done.6
  2.3 0.6 jit_solution_.3.share
  3.0 99.3 %shard_map.170 = (f32[8,128]{1,0:T(8,128)}, f32[160,128]{1,0:T(8,128)}, f32[160,320]{1,0:T(8,128)}, f32[160,320]{1,0:T(8,128)}, f32[160,320]{1,0:T(8,128)}, /*index=5*/f32[160,320]{1,0:T(8,128)}, f32[160,320]{1,0:T(8,128)}) custom-call(f32[8,512]{1,0:T(8,128)} %hist.1, f32[8,128]{1,0:T(8,128)} %later.1, bf16[160,128]{1,0:T(8,128)(2,1)} %fusion.3.eg_in, ...), custom_call_target="tpu_custom_call" | custom-call | tf_op jit(solution)/shard_map/pallas_call | solution.py:723
  102.3 1.2 %slice.9 = f32[1,1]{1,0:T(1,128)} slice(f32[8,128]{1,0:T(8,128)} %get-tuple-element.15), slice={[0:1], [0:1]} | slice | bytes 8 | tf_op jit(solution)/shard_map/slice | solution.py:767
  103.4 1.0 slice_bitcast_fusion
  104.4 0.0 copy-start
  104.4 0.7 copy.22
  105.1 0.2 copy-done
  105.3 0.7 copy.21
  106.0 0.7 copy.28
  106.7 0.3 copy-done.4
  107.0 0.7 copy.29
  107.7 0.3 copy-done.3
  108.1 0.7 copy.30
  108.8 0.3 copy-done.2
  109.1 0.7 copy.31
  109.8 0.3 copy-done.1
  110.1 0.7 copy.32
  (7 shorter events, 0.0 us)
Async XLA Ops:
  0.6 0.8 copy-start.7
  1.6 0.7 copy-start.6
  104.4 0.9 copy-start
  104.4 1.6 %copy-start.5 = (f32[160,320]{1,0:T(8,128)S(1)}, f32[160,320]{1,0:T(8,128)}, u32[]{:S(2)}) copy-start(f32[160,320]{1,0:T(8,128)} %get-tuple-element.41) | copy-start | bytes 614404
  106.0 1.0 copy-start.4
  107.0 1.0 copy-start.3
  108.1 1.0 copy-start.2
  109.1 1.0 copy-start.1

commit v2 on v1

--- a/solution.py
+++ b/solution.py
@@ -280,7 +280,6 @@
     wo_in,
     wh_in,
     pos,
-    share,
     loss_out,
     eg_out,
     q_out,
@@ -337,7 +336,8 @@
     rows = number * PATCHES
     width = pos.shape[1]
     cut = width // dp
-    shard = rows // mp
+    half = rows // 2
+    shard = half // mp
     cols = wq_in.shape[1]
     heads = cols // HEAD_DIM
 
@@ -455,18 +455,22 @@
             total = total + parts_in[i, z_at(-k)].astype(F32)
         return total
 
-    def zg_copy(i, full, k, owner):
-        place = full.at[pl.ds(pl.multiple_of(owner * shard, 16), shard), :]
+    def held(b, owner):
+        return pl.ds(pl.multiple_of(b * half + owner * shard, 16), shard)
+
+    def zg_copy(i, full, b, k, owner):
+        place = full.at[held(b, owner), :]
         return remote(place, place, z_send.at[i, k], z_recv.at[i, k], (me, z_at(k)))
 
-    def zg(i, full, value):
-        full[pl.ds(pl.multiple_of(mz * shard, 16), shard), :] = value
+    def zg(i, full, b, value):
+        full[held(b, mz), :] = value
         for k in range(1, mp):
-            zg_copy(i, full, k, mz).start()
-
-    def zg_finish(i, full):
+            zg_copy(i, full, b, k, mz).start()
+
+    def zg_finish(i, full, b):
         for k in range(1, mp):
-            zg_copy(i, full, k, z_at(-k)).wait_recv()
+            zg_copy(i, full, b, k, z_at(-k)).wait_recv()
+        return full[b * half : (b + 1) * half, :]
 
     inputs = [eg_in, wq_in, wk_in, wv_in, wo_in, wh_in]
     for i, ref in enumerate(inputs):
@@ -536,43 +540,58 @@
         jnp.where((head_lane >= h * HEAD_DIM) & (head_lane < (h + 1) * HEAD_DIM), 1.0, 0.0)
         for h in range(heads)
     ]
-    r_at = lax.broadcasted_iota(jnp.int32, (rows, rows), 0)
-    c_at = lax.broadcasted_iota(jnp.int32, (rows, rows), 1)
+    r_at = lax.broadcasted_iota(jnp.int32, (half, half), 0)
+    c_at = lax.broadcasted_iota(jnp.int32, (half, half), 1)
     causal = (c_at <= r_at) & (c_at >= r_at - (r_at & (PATCHES - 1)))
     scale = 1.0 / math.sqrt(HEAD_DIM)
-    ctx = jnp.zeros((rows, cols), F32)
-    for h in range(heads):
-        scores = mm((q * masks[h]).astype(BF), k_low, (1, 1)) * scale
-        raised = jnp.where(causal, jnp.exp(scores), 0.0)
-        probs = raised / jnp.sum(raised, axis=1, keepdims=True)
-        probs_ref[h] = probs
-        ctx = ctx + mm(probs.astype(BF), (v * masks[h]).astype(BF))
-    ctx_low = ctx.astype(BF)
-    store_own(CTX, ctx_low)
+    spans = [slice(b * half, (b + 1) * half) for b in range(2)]
+    contexts = []
+    for b, span_b in enumerate(spans):
+        ctx = jnp.zeros((half, cols), F32)
+        for h in range(heads):
+            q_head = (q[span_b] * masks[h]).astype(BF)
+            scores = mm(q_head, k_low[span_b], (1, 1)) * scale
+            raised = jnp.where(causal, jnp.exp(scores), 0.0)
+            probs = raised / jnp.sum(raised, axis=1, keepdims=True)
+            probs_ref[b, h] = probs
+            ctx = ctx + mm(probs.astype(BF), (v[span_b] * masks[h]).astype(BF))
+        contexts.append(ctx.astype(BF))
+        if b == 0:
+            ag_finish(WO)
+        rs_start(b, mm(contexts[b], wo_full[...], (1, 1)))
+    store_own(CTX, jnp.concatenate(contexts, axis=0))
     ag_start(CTX)
-    ag_finish(WO)
-    rs_start(0, mm(ctx_low, wo_full[...], (1, 1)))
     ag_finish(WH)
-    shard_rows = pl.ds(pl.multiple_of(mz * shard, 16), shard)
-    rz_shard = rz_ref[shard_rows, :]
-    r1 = rz_shard + rs_finish(0)
-    factor_head = lax.rsqrt(jnp.mean(r1 * r1, axis=1, keepdims=True) + EPS)
-    zg(3, nh_full, (r1 * factor_head * gain_head).astype(BF))
-    zg_finish(3, nh_full)
-    nh = nh_full[...]
-    error = target - mm(nh, wh_full[...])
-    shares = share[0:1, :]
+    rz_shards, r1s, factors = [], [], []
+    for b in range(2):
+        rz_shards.append(rz_ref[held(b, mz), :])
+        r1 = rz_shards[b] + rs_finish(b)
+        factor_head = lax.rsqrt(jnp.mean(r1 * r1, axis=1, keepdims=True) + EPS)
+        zg(6 + b, nh_full, b, (r1 * factor_head * gain_head).astype(BF))
+        r1s.append(r1)
+        factors.append(factor_head)
+    level = lax.broadcasted_iota(jnp.int32, (1, cols), 1).astype(F32)
+    level = level - LEVEL_CHANNELS * jnp.floor((level + 0.5) / LEVEL_CHANNELS)
+    shares = level / LEVEL_CHANNELS
     is_mean = shares == 0.0
-    slope = -error / SMOOTHING_RADIUS
-    small = jnp.exp(-jnp.abs(slope))
-    soft = jnp.maximum(slope, 0.0) + jnp.log1p(small)
-    sig = jnp.where(slope >= 0.0, 1.0, small) / (1.0 + small)
-    terms = jnp.where(is_mean, error * error, shares * error + SMOOTHING_RADIUS * soft)
-    fg = (jnp.where(is_mean, -2.0 * error, sig - shares) / HORIZON_SPAN).astype(BF)
-    store_own(FG, fg)
+    terms = jnp.zeros((half, cols), F32)
+    slopes = []
+    for b, span_b in enumerate(spans):
+        nh = zg_finish(6 + b, nh_full, b)
+        error = target[span_b] - mm(nh, wh_full[...])
+        slope = -error / SMOOTHING_RADIUS
+        small = jnp.exp(-jnp.abs(slope))
+        soft = jnp.maximum(slope, 0.0) + jnp.log1p(small)
+        sig = jnp.where(slope >= 0.0, 1.0, small) / (1.0 + small)
+        terms = terms + jnp.where(
+            is_mean, error * error, shares * error + SMOOTHING_RADIUS * soft
+        )
+        fg = (jnp.where(is_mean, -2.0 * error, sig - shares) / HORIZON_SPAN).astype(BF)
+        slopes.append(fg)
+        rs_start(2 + b, mm(fg, wh_full[...], (1, 1)))
+    store_own(FG, jnp.concatenate(slopes, axis=0))
     ag_start(FG)
-    rs_start(1, mm(fg, wh_full[...], (1, 1)))
-    xx_start(NH, nh.astype(F32).T.astype(BF))
+    xx_start(NH, nh_full[...].astype(F32).T.astype(BF))
     loss_here = jnp.sum(jnp.sum(terms, axis=1, keepdims=True), axis=0, keepdims=True)
     loss_own[...] = jnp.broadcast_to(loss_here, loss_own.shape)
 
@@ -590,35 +609,41 @@
         loss_copy(k, me).start()
     ag_finish(CTX)
 
-    up = rs_finish(1)
-    weighted = gain_head * up
-    inner = jnp.mean(weighted * r1, axis=1, keepdims=True)
-    r1_grad = factor_head * weighted - r1 * factor_head * factor_head * factor_head * inner
-    gain_one = jnp.sum(up * r1 * factor_head, axis=0, keepdims=True)
-    zg(4, al_full, r1_grad.astype(BF))
+    r1_grads = []
+    gain_one = jnp.zeros((1, width), F32)
+    for b in range(2):
+        up = rs_finish(2 + b)
+        r1, factor_head = r1s[b], factors[b]
+        weighted = gain_head * up
+        inner = jnp.mean(weighted * r1, axis=1, keepdims=True)
+        r1_grad = factor_head * weighted - r1 * factor_head * factor_head * factor_head * inner
+        zg(8 + b, al_full, b, r1_grad.astype(BF))
+        r1_grads.append(r1_grad)
+        gain_one = gain_one + jnp.sum(up * r1 * factor_head, axis=0, keepdims=True)
     ag_finish(FG)
-    zg_finish(4, al_full)
-    al = al_full[...]
-    cg = mm(al, wo_full[...])
-    qb = jnp.zeros((rows, cols), F32)
-    kb = jnp.zeros((rows, cols), F32)
-    vb = jnp.zeros((rows, cols), F32)
-    for h in range(heads):
-        cg_head = (cg * masks[h]).astype(BF)
-        probs = probs_ref[h]
-        prob_grad = mm(cg_head, v_low, (1, 1))
-        vb = vb + mm(probs.T.astype(BF), cg_head)
-        centred = prob_grad - jnp.sum(probs * prob_grad, axis=1, keepdims=True)
-        score_grad = probs * centred * scale
-        qb = qb + mm(score_grad.astype(BF), (k_ * masks[h]).astype(BF))
-        kb = kb + mm(score_grad.T.astype(BF), (q * masks[h]).astype(BF))
-    qb, kb, vb = qb.astype(BF), kb.astype(BF), vb.astype(BF)
-    for i, value in ((QB, qb), (KB, kb), (VB, vb)):
-        store_own(i, value)
+    backs = []
+    for b, span_b in enumerate(spans):
+        cg = mm(zg_finish(8 + b, al_full, b), wo_full[...])
+        qb = jnp.zeros((half, cols), F32)
+        kb = jnp.zeros((half, cols), F32)
+        vb = jnp.zeros((half, cols), F32)
+        for h in range(heads):
+            cg_head = (cg * masks[h]).astype(BF)
+            probs = probs_ref[b, h]
+            prob_grad = mm(cg_head, v_low[span_b], (1, 1))
+            vb = vb + mm(probs.T.astype(BF), cg_head)
+            centred = prob_grad - jnp.sum(probs * prob_grad, axis=1, keepdims=True)
+            score_grad = probs * centred * scale
+            qb = qb + mm(score_grad.astype(BF), (k_[span_b] * masks[h]).astype(BF))
+            kb = kb + mm(score_grad.T.astype(BF), (q[span_b] * masks[h]).astype(BF))
+        qb, kb, vb = qb.astype(BF), kb.astype(BF), vb.astype(BF)
+        backs.append((qb, kb, vb))
+        back = mm(qb, wq_full[...], (1, 1)) + mm(kb, wk_full[...], (1, 1))
+        rs_start(4 + b, back + mm(vb, wv_full[...], (1, 1)))
+    for n, i in enumerate((QB, KB, VB)):
+        store_own(i, jnp.concatenate([backs[0][n], backs[1][n]], axis=0))
         ag_start(i)
-    back = mm(qb, wq_full[...], (1, 1)) + mm(kb, wk_full[...], (1, 1))
-    rs_start(2, back + mm(vb, wv_full[...], (1, 1)))
-    xx_start(AL, al.astype(F32).T.astype(BF))
+    xx_start(AL, al_full[...].astype(F32).T.astype(BF))
 
     total = loss_own[...]
     for k in range(1, dp):
@@ -630,18 +655,25 @@
     xx_finish(NH)
     h_out[...] = mm(nh_all[...], fg_full[...])
 
-    up = rs_finish(2)
-    factor = lax.rsqrt(jnp.mean(rz_shard * rz_shard, axis=1, keepdims=True) + EPS)
-    weighted = gain_attn * up
-    inner = jnp.mean(weighted * rz_shard, axis=1, keepdims=True)
-    rz_grad = r1_grad + (factor * weighted - rz_shard * factor * factor * factor * inner)
-    gain_zero = jnp.sum(up * rz_shard * factor, axis=0, keepdims=True)
+    rz_grads = []
+    gain_zero = jnp.zeros((1, width), F32)
+    for b in range(2):
+        up = rs_finish(4 + b)
+        rz_shard = rz_shards[b]
+        factor = lax.rsqrt(jnp.mean(rz_shard * rz_shard, axis=1, keepdims=True) + EPS)
+        weighted = gain_attn * up
+        inner = jnp.mean(weighted * rz_shard, axis=1, keepdims=True)
+        rz_grads.append(
+            r1_grads[b] + (factor * weighted - rz_shard * factor * factor * factor * inner)
+        )
+        gain_zero = gain_zero + jnp.sum(up * rz_shard * factor, axis=0, keepdims=True)
     which = lax.broadcasted_iota(jnp.int32, (16, width), 0)
     both = jnp.where(which == 0, gain_zero, jnp.where(which == 1, gain_one, 0.0))
     both_high = both.astype(BF).astype(F32)
-    stacked = jnp.concatenate([rz_grad, both_high, both - both_high], axis=0)
+    stacked = jnp.concatenate([*rz_grads, both_high, both - both_high], axis=0)
     hot = jnp.where(pick == PATCH, 1.0, 0.0)
-    other = jnp.concatenate([patch_ref[shard_rows, :].astype(F32), hot, hot], axis=0)
+    mine = [patch_ref[held(b, mz), :].astype(F32) for b in range(2)]
+    other = jnp.concatenate([*mine, hot, hot], axis=0)
     xx_start(EP, mm(stacked.T.astype(BF), other.astype(BF)).astype(BF))
 
     total = loss_mid[...]
@@ -659,7 +691,7 @@
     egz_own[...] = summed.astype(BF)
 
     def egz(k, sender):
-        return remote(egz_own, egz_all.at[sender], z_send.at[5, k], z_recv.at[5, k], (me, z_at(k)))
+        return remote(egz_own, egz_all.at[sender], z_send.at[10, k], z_recv.at[10, k], (me, z_at(k)))
 
     for k in range(1, mp):
         egz(k, mz).start()
@@ -683,12 +715,26 @@
     for k in range(1, dp):
         loss_copy(k, me).wait_send()
     for k in range(1, mp):
-        for i in range(3):
+        for i in range(6):
             rs_copy(i, k, mz, z_at(k)).wait_send()
-        zg_copy(3, nh_full, k, mz).wait_send()
-        zg_copy(4, al_full, k, mz).wait_send()
+        for b in range(2):
+            zg_copy(6 + b, nh_full, b, k, mz).wait_send()
+            zg_copy(8 + b, al_full, b, k, mz).wait_send()
         egz(k, mz).wait_send()
         loss_z(k, mz).wait_send()
+
+
+def placing_kernel(lift, gains, loss, small, q, k, v, o, h, *outs):
+    loss_out, lift_out, gains_out, q_out, k_out, v_out, o_out, h_out = outs
+    loss_out[0, 0] = loss[0, 0]
+    turned = small[...].T
+    lift_out[...] = turned[:lift]
+    gains_out[...] = turned[lift : lift + gains]
+    q_out[...] = q[...]
+    k_out[...] = k[...]
+    v_out[...] = v[...]
+    o_out[...] = o[...]
+    h_out[...] = h[...]
 
 
 def fused_device(
@@ -710,24 +756,23 @@
     width = cut * dp
     small = jnp.concatenate([patch_lift_matrix, scaling_factors], axis=0)
     small = jnp.pad(small, ((0, 128 - small.shape[0]), (0, 0))).T
-    levels = np.arange(cols) % LEVEL_CHANNELS
-    share = np.broadcast_to((levels.astype(np.float32) / LEVEL_CHANNELS)[None], (8, cols))
     vmem = pltpu.VMEM
     full = vmem((width, cols), BF)
     tall = vmem((rows * dp, cols), BF)
     across = vmem((cut, rows * dp), BF)
     dma = pltpu.SemaphoreType.DMA
     grad = jax.ShapeDtypeStruct((cut, cols), F32)
-    shard = rows // mp
+    half = rows // 2
+    shard = half // mp
     chips = dp // 2
-    loss, small_grad, query_grad, key_grad, value_grad, output_grad, head_grad = pl.pallas_call(
+    results = pl.pallas_call(
         functools.partial(sublayer_kernel, (dp, mp)),
         out_shape=(
             jax.ShapeDtypeStruct((8, 128), F32),
             jax.ShapeDtypeStruct((cut, 128), F32),
             grad, grad, grad, grad, grad,
         ),
-        in_specs=[pl.BlockSpec(memory_space=vmem)] * 10,
+        in_specs=[pl.BlockSpec(memory_space=vmem)] * 9,
         out_specs=(pl.BlockSpec(memory_space=vmem),) * 7,
         scratch_shapes=[
             vmem((width, 128), BF), full, full, full, full, full,
@@ -735,13 +780,13 @@
             vmem((4, width, rows), BF),
             across, across, across,
             vmem((dp, cut, rows), BF),
-            vmem((3, rows, width), BF),
-            vmem((3, mp, shard, width), BF),
+            vmem((6, half, width), BF),
+            vmem((6, mp, shard, width), BF),
             vmem((rows, width), BF),
             vmem((rows, width), BF),
             vmem((rows, width), F32),
             vmem((rows, 128), BF),
-            vmem((cols // HEAD_DIM, rows, rows), F32),
+            vmem((2, cols // HEAD_DIM, half, half), F32),
             vmem((cut, 128), BF),
             vmem((mp, cut, 128), BF),
             vmem((8, 128), F32),
@@ -750,7 +795,7 @@
             vmem((mp, 8, 128), F32),
             dma((11, 2 * chips - 1)), dma((11, 2 * chips - 1)),
             dma((4, dp)), dma((4, dp)),
-            dma((6, mp)), dma((6, mp)),
+            dma((11, mp)), dma((11, mp)),
             dma((2, max(dp, mp))), dma((2, max(dp, mp))),
         ],
         compiler_params=pltpu.CompilerParams(
@@ -759,20 +804,23 @@
     )(
         history_sequences, later_steps, small, asking_matrix, lookup_matrix, content_matrix,
         attend_exit_matrix.T, outlook_matrix,
-        jnp.asarray(position_table(PATCHES, width)), jnp.asarray(share),
+        jnp.asarray(position_table(PATCHES, width)),
     )
     lift = patch_lift_matrix.shape[0]
     gains = scaling_factors.shape[0]
-    return (
-        loss[0, 0],
-        small_grad[:, :lift].T,
-        small_grad[:, lift : lift + gains].T,
-        query_grad,
-        key_grad,
-        value_grad,
-        output_grad.T,
-        head_grad,
-    )
+    space = pl.BlockSpec(memory_space=vmem)
+    loss, *grads = pl.pallas_call(
+        functools.partial(placing_kernel, lift, gains),
+        out_shape=(
+            jax.ShapeDtypeStruct((1, 1), F32),
+            jax.ShapeDtypeStruct((lift, cut), F32),
+            jax.ShapeDtypeStruct((gains, cut), F32),
+            grad, grad, grad, grad, grad,
+        ),
+        in_specs=[space] * 7,
+        out_specs=(pl.BlockSpec(memory_space=pltpu.SMEM), *([space] * 7)),
+    )(*results)
+    return (loss.reshape(()), *grads[:5], grads[5].T, grads[6])
 
 
 def fits(dp, mp, arrays):
@@ -784,7 +832,7 @@
         and dp > 2
         and mp > 1
         and cut % 16 == 0
-        and rows % (16 * mp) == 0
+        and rows % (32 * mp) == 0
         and cols % HEAD_DIM == 0
         and cols == PATCH * LEVEL_CHANNELS
     )

time: 111 us -> 102 us (0.919)
  local copies, waits for them, and re-layouts: 10.1 us -> 0.98 us
    unnamed x25 -> x4, local copies, waits for them, and re-layouts: 7.38 us -> 0.98 us
    pallas_call x0 -> x1, Pallas kernels: none -> 2.45 us  [fused_device(): pl.pallas_call(functools.partial(placing_kernel, lift, gains), out_shape=...]
    pallas_call x1, Pallas kernels: 99.3 us -> 96.9 us  [fused_device(): pl.pallas_call(functools.partial(sublayer_kernel, (dp, mp)), out_shape=(j...]
    slice x1 -> x0, local copies, waits for them, and re-layouts: 1.19 us -> none  [fused_device(): loss[0, 0]]
where the time goes in v2:
time: 102 us
  Pallas kernels  99.3 us (97%)
    pallas_call x1, Pallas kernels, fused_device(): pl.pallas_call(functools.partial(sublayer_kernel, (dp, mp)), out_shape=(j...  96.9 us
    pallas_call x1, Pallas kernels, fused_device(): pl.pallas_call(functools.partial(placing_kernel, lift, gains), out_shape=...  2.45 us

profile of v2, /device:TPU:0, one launch (start us, length us, event | category | flops | bytes accessed | tf_op | source)
XLA Modules:
  0.0 101.7 jit_solution(13720384187759660449)
XLA Ops:
  0.6 0.0 copy-start
  0.6 0.8 copy.18
  1.5 0.0 copy-done
  1.5 0.1 copy.19
  1.6 0.7 fusion.3.eg_in
  2.3 96.9 %shard_map.161 = (f32[8,128]{1,0:T(8,128)}, f32[160,128]{1,0:T(8,128)}, f32[160,320]{1,0:T(8,128)}, f32[160,320]{1,0:T(8,128)}, f32[160,320]{1,0:T(8,128)}, /*index=5*/f32[160,320]{1,0:T(8,128)}, f32[160,320]{1,0:T(8,128)}) custom-call(f32[8,512]{1,0:T(8,128)} %hist.1, f32[8,128]{1,0:T(8,128)} %later.1, bf16[160,128]{1,0:T(8,128)(2,1)} %fusion.3.eg_in, ...), custom_call_target="tpu_custom_call" | custom-call | tf_op jit(solution)/shard_map/pallas_call | solution.py:768
  99.2 2.4 %shard_map.162 = (f32[1,1]{1,0:T(1,128)}, f32[32,160]{1,0:T(8,128)}, f32[2,160]{1,0:T(2,128)}, f32[160,320]{1,0:T(8,128)}, f32[160,320]{1,0:T(8,128)}, /*index=5...) custom-call(f32[8,128]{1,0:T(8,128)} %get-tuple-element.23.loss, f32[160,128]{1,0:T(8,128)} %get-tuple-element.24.small, ...), custom_call_target="tpu_custom_call" | custom-call | tf_op jit(solution)/shard_map/pallas_call | solution.py:812
Async XLA Ops:
  0.6 0.8 copy-start

commit v3 on v2

--- a/solution.py
+++ b/solution.py
@@ -561,7 +561,6 @@
         rs_start(b, mm(contexts[b], wo_full[...], (1, 1)))
     store_own(CTX, jnp.concatenate(contexts, axis=0))
     ag_start(CTX)
-    ag_finish(WH)
     rz_shards, r1s, factors = [], [], []
     for b in range(2):
         rz_shards.append(rz_ref[held(b, mz), :])
@@ -570,6 +569,7 @@
         zg(6 + b, nh_full, b, (r1 * factor_head * gain_head).astype(BF))
         r1s.append(r1)
         factors.append(factor_head)
+    ag_finish(WH)
     level = lax.broadcasted_iota(jnp.int32, (1, cols), 1).astype(F32)
     level = level - LEVEL_CHANNELS * jnp.floor((level + 0.5) / LEVEL_CHANNELS)
     shares = level / LEVEL_CHANNELS
@@ -620,10 +620,12 @@
         zg(8 + b, al_full, b, r1_grad.astype(BF))
         r1_grads.append(r1_grad)
         gain_one = gain_one + jnp.sum(up * r1 * factor_head, axis=0, keepdims=True)
-    ag_finish(FG)
     backs = []
     for b, span_b in enumerate(spans):
-        cg = mm(zg_finish(8 + b, al_full, b), wo_full[...])
+        al = zg_finish(8 + b, al_full, b)
+        if b == 1:
+            xx_start(AL, al_full[...].astype(F32).T.astype(BF))
+        cg = mm(al, wo_full[...])
         qb = jnp.zeros((half, cols), F32)
         kb = jnp.zeros((half, cols), F32)
         vb = jnp.zeros((half, cols), F32)
@@ -643,7 +645,7 @@
     for n, i in enumerate((QB, KB, VB)):
         store_own(i, jnp.concatenate([backs[0][n], backs[1][n]], axis=0))
         ag_start(i)
-    xx_start(AL, al_full[...].astype(F32).T.astype(BF))
+    ag_finish(FG)
 
     total = loss_own[...]
     for k in range(1, dp):

time: 102 us -> 99.9 us (0.979)
  Pallas kernels: 99.3 us -> 97.2 us
    pallas_call x1, Pallas kernels: 96.9 us -> 94.8 us  [fused_device(): pl.pallas_call(functools.partial(sublayer_kernel, (dp, mp)), out_shape=(j...]
where the time goes in v3:
time: 99.9 us; the launch traced here: 99.6 us
  Pallas kernels  97.2 us (97%)
    pallas_call x1, Pallas kernels, fused_device(): pl.pallas_call(functools.partial(sublayer_kernel, (dp, mp)), out_shape=(j...  94.8 us
    pallas_call x1, Pallas kernels, fused_device(): pl.pallas_call(functools.partial(placing_kernel, lift, gains), out_shape=...  2.45 us

profile of v3, /device:TPU:0, one launch (start us, length us, event | category | flops | bytes accessed | tf_op | source)
XLA Modules:
  0.0 99.6 jit_solution(11928581650716859194)
XLA Ops:
  0.6 0.0 copy-start
  0.6 0.8 copy.18
  1.5 0.0 copy-done
  1.5 0.1 copy.19
  1.6 0.7 fusion.3.eg_in
  2.3 94.8 %shard_map.161 = (f32[8,128]{1,0:T(8,128)}, f32[160,128]{1,0:T(8,128)}, f32[160,320]{1,0:T(8,128)}, f32[160,320]{1,0:T(8,128)}, f32[160,320]{1,0:T(8,128)}, /*index=5*/f32[160,320]{1,0:T(8,128)}, f32[160,320]{1,0:T(8,128)}) custom-call(f32[8,512]{1,0:T(8,128)} %hist.1, f32[8,128]{1,0:T(8,128)} %later.1, bf16[160,128]{1,0:T(8,128)(2,1)} %fusion.3.eg_in, ...), custom_call_target="tpu_custom_call" | custom-call | tf_op jit(solution)/shard_map/pallas_call | solution.py:770
  97.1 2.4 %shard_map.162 = (f32[1,1]{1,0:T(1,128)}, f32[32,160]{1,0:T(8,128)}, f32[2,160]{1,0:T(2,128)}, f32[160,320]{1,0:T(8,128)}, f32[160,320]{1,0:T(8,128)}, /*index=5...) custom-call(f32[8,128]{1,0:T(8,128)} %get-tuple-element.23.loss, f32[160,128]{1,0:T(8,128)} %get-tuple-element.24.small, ...), custom_call_target="tpu_custom_call" | custom-call | tf_op jit(solution)/shard_map/pallas_call | solution.py:814
Async XLA Ops:
  0.6 0.8 copy-start
